TPU v7x, 256 devices: a whole 4x4x8 slice. The times are simulated.
256 devices in a mesh: af: 4 (over y), sa: 64 (over z, x, core).
Axes of the slice: x: 4, y: 4, z: 8, core: 2. Of those that a mesh axis runs over, the one named last changes fastest.
Arguments:
- data_real: bfloat16 [64, 512, 512], P('af', 'sa'), may hold values from -0.5 to 0.5
- data_imaginary: bfloat16 [64, 512, 512], P('af', 'sa'), may hold values from -0.5 to 0.5
- wavelet_real: float32 [64], P('af'), may hold values from -2.5 to 2.5
- wavelet_imaginary: float32 [64], P('af'), may hold values from -2.5 to 2.5
- primaries_real: float32 [64, 512, 512], P('af', 'sa'), may hold values from -3 to 3
- primaries_imaginary: float32 [64, 512, 512], P('af', 'sa'), may hold values from -3 to 3
Outputs:
- updated_real: float32 [64, 512, 512], P('af', 'sa')
- updated_imaginary: float32 [64, 512, 512], P('af', 'sa')
- misfit: float32 [2], replicated
All inputs are finite; a program needn't handle non-finite values.
Results may differ from a plain program's by a relative error of at most 0.0018.
Values may be sent and summed in bfloat16 or wider, within the bound.
A program may use at most 64 MiB of HBM per device.

v0:
```python
import math
import jax
import jax.numpy as jnp
from jax import lax
from jax.sharding import Mesh
from jax.sharding import PartitionSpec as P

N = 512
F = 64
ITERS = 2
SA = ("sa_0", "sa_1", "sa_2")
AF_SA = ("af", "sa_0", "sa_1", "sa_2")
STEP_LENGTH = 0.02
THRESHOLD = 0.25


def side_by_side(arrays, axis, dim, along):
    both = jnp.concatenate(arrays, axis=along)
    result, at, finished = (lax.all_gather(both, axis, axis=dim, tiled=True), 0, [])
    for a in arrays:
        finished.append(lax.slice_in_dim(result, at, at + a.shape[along], axis=along))
        at += a.shape[along]
    return tuple(finished)


def in_one_piece(arrays, axis, split_dim, concat_dim, along):
    widths = [a.shape[along] for a in arrays]
    both = jnp.concatenate(arrays, axis=along)
    result = lax.all_to_all(both, axis, split_axis=split_dim, concat_axis=concat_dim, tiled=True)
    return tuple(jnp.split(result, [sum(widths[:k]) for k in range(1, len(widths))], axis=along))


def by_axis(value, axes):
    for axis in axes:
        value = lax.psum(value, axis)
    return value


def fourier_tables(row_index, col_index):
    phase = row_index[:, None] * col_index[None, :] % F
    angle = phase.astype(jnp.float32) * (2.0 * math.pi / F)
    factor = 1.0 / math.sqrt(F)
    return (jnp.cos(angle) * factor, jnp.sin(angle) * factor)


def highest(left, right):
    return jnp.dot(left, right, precision=lax.Precision.HIGHEST, preferred_element_type=jnp.float32)


def stacked(part_real, part_imaginary):
    return jnp.concatenate(
        [part_real.astype(jnp.bfloat16), part_imaginary.astype(jnp.bfloat16)], axis=1
    )


def shrink(values):
    return values - jnp.clip(values, -THRESHOLD, THRESHOLD)


def on_device(
    data_real, data_imaginary, wavelet_real, wavelet_imaginary, primaries_real, primaries_imaginary
):
    row_count = data_real.shape[1]
    wave_real = wavelet_real[:, None, None]
    wave_imaginary = wavelet_imaginary[:, None, None]
    current_real = primaries_real
    current_imaginary = primaries_imaginary
    own_real = data_real.astype(jnp.float32)
    own_imaginary = data_imaginary.astype(jnp.float32)
    whole_real, whole_imaginary = side_by_side((data_real, data_imaginary), SA, 1, 0)
    local_sums = []
    for iteration in range(ITERS):
        left_rows = stacked(current_real, current_imaginary)
        product_real = jnp.einsum(
            "frk,fkc->frc", left_rows, whole_real, preferred_element_type=jnp.float32
        )
        product_imaginary = jnp.einsum(
            "frk,fkc->frc", left_rows, whole_imaginary, preferred_element_type=jnp.float32
        )
        forward_real = product_real[:, :row_count] - product_imaginary[:, row_count:]
        forward_imaginary = product_imaginary[:, :row_count] + product_real[:, row_count:]
        error_real = (
            own_real
            + forward_real
            - (wave_real * current_real - wave_imaginary * current_imaginary)
        )
        error_imaginary = (
            own_imaginary
            + forward_imaginary
            - (wave_real * current_imaginary + wave_imaginary * current_real)
        )
        local_sum = jnp.sum(error_real * error_real) + jnp.sum(error_imaginary * error_imaginary)
        local_sums.append(local_sum)
        error_rows = stacked(error_real, error_imaginary)
        with_real = jnp.einsum(
            "frk,fjk->frj", error_rows, whole_real, preferred_element_type=jnp.float32
        )
        with_imaginary = jnp.einsum(
            "frk,fjk->frj", error_rows, whole_imaginary, preferred_element_type=jnp.float32
        )
        back_real = with_real[:, :row_count] + with_imaginary[:, row_count:]
        back_imaginary = with_real[:, row_count:] - with_imaginary[:, :row_count]
        gradient_real = wave_real * error_real + wave_imaginary * error_imaginary - back_real
        gradient_imaginary = (
            wave_real * error_imaginary - wave_imaginary * error_real - back_imaginary
        )
        stepped_real = current_real + STEP_LENGTH * gradient_real
        stepped_imaginary = current_imaginary + STEP_LENGTH * gradient_imaginary
        trace_real, trace_imaginary = (
            lax.all_to_all(stepped_real, "af", split_axis=2, concat_axis=0, tiled=True),
            lax.all_to_all(stepped_imaginary, "af", split_axis=2, concat_axis=0, tiled=True),
        )
        block_shape = trace_real.shape
        flat_real = trace_real.reshape(F, -1)
        flat_imaginary = trace_imaginary.reshape(F, -1)
        every_index = jnp.arange(F, dtype=jnp.int32)
        cosine, sine = fourier_tables(every_index, every_index)
        time_real = highest(cosine, flat_real) - highest(sine, flat_imaginary)
        time_imaginary = highest(sine, flat_real) + highest(cosine, flat_imaginary)
        shrunk_real = shrink(time_real)
        shrunk_imaginary = shrink(time_imaginary)
        freq_real = (highest(cosine, shrunk_real) + highest(sine, shrunk_imaginary)).reshape(
            block_shape
        )
        freq_imaginary = (highest(cosine, shrunk_imaginary) - highest(sine, shrunk_real)).reshape(
            block_shape
        )
        current_real, current_imaginary = in_one_piece((freq_real, freq_imaginary), "af", 0, 2, 1)
    totals = by_axis(jnp.stack(local_sums), AF_SA)
    misfit = totals / (F * N * N)
    return (current_real, current_imaginary, misfit)


def solution(mesh):
    split = Mesh(mesh.devices.reshape(mesh.shape["af"], 8, 4, 2), ("af", "sa_0", "sa_1", "sa_2"))
    in_specs = (
        P("af", SA, None),
        P("af", SA, None),
        P("af"),
        P("af"),
        P("af", SA, None),
        P("af", SA, None),
    )
    out_specs = (P("af", SA, None), P("af", SA, None), P())
    return jax.shard_map(
        on_device, mesh=split, in_specs=in_specs, out_specs=out_specs, check_vma=False
    )
```

profile of v0, /device:TPU:1, one launch (start us, length us, event | category | flops | bytes accessed | tf_op | source)
XLA Modules:
  0.0 275.2 jit_solution(14884716040026939522)
XLA Ops:
  7.2 1.7 pad_maximum_fusion.3
  11.0 110.2 %all-gather.2.cloned.1.call-done = bf16[32,512,512]{2,1,0:T(8,128)(2,1)} async-done(((bf16[32,8,512]{2,1,0:T(8,128)(2,1)}), bf16[32,512,512]{2,1,0:T(8,128)(2,1)}) %all-gather.2.cloned.1.call-update) | async-done | bytes 16777232 | tf_op jit(solution)/shard_map/all_gather | solution.py:19
  121.1 4.7 %fusion.6 = f32[16,16,512]{2,1,0:T(8,128)S(1)} fusion(bf16[32,512,512]{2,1,0:T(8,128)(2,1)} %all-gather.2.cloned.1.call-done, bf16[16,8,512]{2,1,0:T(8,128)(2,1)S(1)} %convert_element_type.67, bf16[16,8,512]{2,1,0:T(8,128)(2,1)S(1)} %convert_element_type.66), kind=kOutput, calls=%fused_computation.6 | convolution fusion | flops 134742016 | bytes 9175040 | tf_op jit(solution)/shard_map/frk,fkc->frc/dot_general | solution.py:77
  125.9 5.3 %fusion.14 = f32[16,16,512]{2,1,0:T(8,128)S(1)} fusion(bf16[32,512,512]{2,1,0:T(8,128)(2,1)} %all-gather.2.cloned.1.call-done, bf16[16,8,512]{2,1,0:T(8,128)(2,1)S(1)} %convert_element_type.67, bf16[16,8,512]{2,1,0:T(8,128)(2,1)S(1)} %convert_element_type.66), kind=kOutput, calls=%fused_computation.14 | convolution fusion | flops 134742016 | bytes 9175040 | tf_op jit(solution)/shard_map/frk,fkc->frc/dot_general | solution.py:74
  132.1 2.3 fusion.4
  134.4 2.3 fusion.12
  137.8 1.5 reshape.44
  139.2 4.0 %all-to-all-start = ((f32[4,1,16384]{2,1,0:T(1,128)}), f32[4,1,16384]{2,1,0:T(1,128)S(1)}, u32[]{:S(2)}, u32[]{:S(2)}) async-start(f32[4,1,16384]{2,1,0:T(1,128)} %reshape.44), calls=%async_computation | async-start | bytes 524288 | tf_op jit(solution)/shard_map/all_to_all | solution.py:110
  145.5 3.6 %all-to-all-done = f32[4,1,16384]{2,1,0:T(1,128)S(1)} async-done(((f32[4,1,16384]{2,1,0:T(1,128)}), f32[4,1,16384]{2,1,0:T(1,128)S(1)}, u32[]{:S(2)}, u32[]{:S(2)}) %all-to-all-start) | async-done | bytes 262176 | tf_op jit(solution)/shard_map/all_to_all | solution.py:110
  149.1 3.6 %all-to-all-start.1 = ((f32[4,1,16384]{2,1,0:T(1,128)}), f32[4,1,16384]{2,1,0:T(1,128)S(1)}, u32[]{:S(2)}, u32[]{:S(2)}) async-start(f32[4,1,16384]{2,1,0:T(1,128)} %reshape.46), calls=%async_computation.1 | async-start | bytes 524288 | tf_op jit(solution)/shard_map/all_to_all | solution.py:111
  164.0 9.7 %all_to_all.96 = f32[64,16,128]{2,1,0:T(8,128)S(1)} all-to-all(f32[64,16,128]{2,1,0:T(8,128)S(1)} %pad_maximum_fusion), channel_id=1, replica_groups=mesh['af'=4,'sa_0'=8,'sa_1'=4,'sa_2'=2] {'af'}, dimensions={0} | all-to-all | bytes 1048576 | tf_op jit(solution)/shard_map/all_to_all | solution.py:29
  173.9 4.7 %fusion.2 = f32[16,16,512]{2,1,0:T(8,128)S(1)} fusion(bf16[32,512,512]{2,1,0:T(8,128)(2,1)} %all-gather.2.cloned.1.call-done, bf16[16,8,512]{2,1,0:T(8,128)(2,1)S(1)} %get-tuple-element.22, bf16[16,8,512]{2,1,0:T(8,128)(2,1)S(1)} %get-tuple-element.21), kind=kOutput, calls=%fused_computation.2 | convolution fusion | flops 134742016 | bytes 9175040 | tf_op jit(solution)/shard_map/frk,fkc->frc/dot_general | solution.py:77
  178.6 4.7 %fusion.10 = f32[16,16,512]{2,1,0:T(8,128)S(1)} fusion(bf16[32,512,512]{2,1,0:T(8,128)(2,1)} %all-gather.2.cloned.1.call-done, bf16[16,8,512]{2,1,0:T(8,128)(2,1)S(1)} %get-tuple-element.22, bf16[16,8,512]{2,1,0:T(8,128)(2,1)S(1)} %get-tuple-element.21), kind=kOutput, calls=%fused_computation.10 | convolution fusion | flops 134742016 | bytes 9175040 | tf_op jit(solution)/shard_map/frk,fkc->frc/dot_general | solution.py:74
  184.3 2.3 fusion
  186.6 2.3 fusion.8
  191.4 3.4 %all-to-all-start.3 = ((f32[4,1,16384]{2,1,0:T(1,128)}), f32[4,1,16384]{2,1,0:T(1,128)S(1)}, u32[]{:S(2)}, u32[]{:S(2)}) async-start(f32[4,1,16384]{2,1,0:T(1,128)} %reshape.48), calls=%async_computation.3 | async-start | bytes 524288 | tf_op jit(solution)/shard_map/all_to_all | solution.py:110
  197.1 3.2 %all-to-all-done.3 = f32[4,1,16384]{2,1,0:T(1,128)S(1)} async-done(((f32[4,1,16384]{2,1,0:T(1,128)}), f32[4,1,16384]{2,1,0:T(1,128)S(1)}, u32[]{:S(2)}, u32[]{:S(2)}) %all-to-all-start.3) | async-done | bytes 262176 | tf_op jit(solution)/shard_map/all_to_all | solution.py:110
  200.3 3.7 %all-to-all-start.4 = ((f32[4,1,16384]{2,1,0:T(1,128)}), f32[4,1,16384]{2,1,0:T(1,128)S(1)}, u32[]{:S(2)}, u32[]{:S(2)}) async-start(f32[4,1,16384]{2,1,0:T(1,128)} %reshape.50), calls=%async_computation.4 | async-start | bytes 524288 | tf_op jit(solution)/shard_map/all_to_all | solution.py:111
  207.7 1.5 all-to-all-done.4
  216.0 3.5 %all-to-all-start.5 = ((f32[64,16,128]{2,1,0:T(8,128)}), f32[64,16,128]{2,1,0:T(8,128)S(1)}, u32[]{:S(2)}, u32[]{:S(2)}) async-start(f32[64,16,128]{2,1,0:T(8,128)} %pad_maximum_fusion.1), calls=%async_computation.5 | async-start | bytes 1048576 | tf_op jit(solution)/shard_map/all_to_all | solution.py:29
  222.0 9.3 %psum.28 = f32[2]{0:T(128)S(1)} all-reduce(f32[2]{0:T(128)S(1)} %pad_maximum_fusion.15), channel_id=1, replica_groups=mesh['af'=4,'sa_0'=8,'sa_1'=4,'sa_2'=2] {'af'}, use_global_device_ids=true, to_apply=%region_4.5 | all-reduce | flops 2 | bytes 16 | tf_op jit(solution)/shard_map/psum | solution.py:35
  231.3 12.5 %psum.29 = f32[2]{0:T(128)S(1)} all-reduce(f32[2]{0:T(128)S(1)} %psum.28), channel_id=1, replica_groups=mesh['af'=4,'sa_0'=8,'sa_1'=4,'sa_2'=2] {'sa_0'}, use_global_device_ids=true, to_apply=%region_5.6 | all-reduce | flops 2 | bytes 16 | tf_op jit(solution)/shard_map/psum | solution.py:35
  243.8 7.2 %psum.30 = f32[2]{0:T(128)S(1)} all-reduce(f32[2]{0:T(128)S(1)} %psum.29), channel_id=1, replica_groups=mesh['af'=4,'sa_0'=8,'sa_1'=4,'sa_2'=2] {'sa_1'}, use_global_device_ids=true, to_apply=%region_6.7 | all-reduce | flops 2 | bytes 16 | tf_op jit(solution)/shard_map/psum | solution.py:35
  251.1 15.4 %psum.31 = f32[2]{0:T(128)S(1)} all-reduce(f32[2]{0:T(128)S(1)} %psum.30), channel_id=1, replica_groups=mesh['af'=4,'sa_0'=8,'sa_1'=4,'sa_2'=2] {'sa_2'}, use_global_device_ids=true, to_apply=%region_7.8 | all-reduce | flops 2 | bytes 16 | tf_op jit(solution)/shard_map/psum | solution.py:35
  (86 shorter events, 35.6 us)
Async XLA Ops:
  7.2 114.0 %all-gather.2.cloned.1.call-start = ((), (), s32[]{:S(2)}) async-start(), calls=%async_computation.6 | async-start | bytes 17039360 | tf_op jit(solution)/shard_map/all_gather | solution.py:19
  10.9 120.3 %copy-start.1 = (f32[16,8,512]{2,1,0:T(8,128)S(1)}, f32[16,8,512]{2,1,0:T(8,128)}, u32[]{:S(2)}) copy-start(f32[16,8,512]{2,1,0:T(8,128)} %param.11) | copy-start | bytes 786436
  10.9 120.3 %copy-start.2 = (f32[16,8,512]{2,1,0:T(8,128)S(1)}, f32[16,8,512]{2,1,0:T(8,128)}, u32[]{:S(2)}) copy-start(f32[16,8,512]{2,1,0:T(8,128)} %param.10) | copy-start | bytes 786436
  10.9 120.3 %copy-start.3 = (bf16[16,8,512]{2,1,0:T(8,128)(2,1)S(1)}, bf16[16,8,512]{2,1,0:T(8,128)(2,1)}, u32[]{:S(2)}) copy-start(bf16[16,8,512]{2,1,0:T(8,128)(2,1)} %param.7) | copy-start | bytes 393220
  10.9 120.3 %copy-start.4 = (bf16[16,8,512]{2,1,0:T(8,128)(2,1)S(1)}, bf16[16,8,512]{2,1,0:T(8,128)(2,1)}, u32[]{:S(2)}) copy-start(bf16[16,8,512]{2,1,0:T(8,128)(2,1)} %param.6) | copy-start | bytes 393220
  10.9 120.3 %copy-start.5 = (f32[16]{0:T(128)S(1)}, f32[16]{0:T(128)}, u32[]{:S(2)}) copy-start(f32[16]{0:T(128)} %param.9) | copy-start | bytes 196
  10.9 120.3 %copy-start.6 = (f32[16]{0:T(128)S(1)}, f32[16]{0:T(128)}, u32[]{:S(2)}) copy-start(f32[16]{0:T(128)} %param.8) | copy-start | bytes 196
  121.1 11.0 %copy-start = (bf16[32,512,512]{2,1,0:T(8,128)(2,1)S(1)}, bf16[32,512,512]{2,1,0:T(8,128)(2,1)}, u32[]{:S(2)}) copy-start(bf16[32,512,512]{2,1,0:T(8,128)(2,1)} %all-gather.2.cloned.1.call-done) | copy-start | bytes 50331652
  139.2 9.9 %all-to-all-start = ((f32[4,1,16384]{2,1,0:T(1,128)}), f32[4,1,16384]{2,1,0:T(1,128)S(1)}, u32[]{:S(2)}, u32[]{:S(2)}) async-start(f32[4,1,16384]{2,1,0:T(1,128)} %reshape.44), calls=%async_computation | async-start | bytes 524288 | tf_op jit(solution)/shard_map/all_to_all | solution.py:110
  149.1 8.9 %all-to-all-start.1 = ((f32[4,1,16384]{2,1,0:T(1,128)}), f32[4,1,16384]{2,1,0:T(1,128)S(1)}, u32[]{:S(2)}, u32[]{:S(2)}) async-start(f32[4,1,16384]{2,1,0:T(1,128)} %reshape.46), calls=%async_computation.1 | async-start | bytes 524288 | tf_op jit(solution)/shard_map/all_to_all | solution.py:111
  160.7 23.6 %slice-start = ((s8[16777216]{0:T(1024)(128)(4,1)}), s8[4194304]{0:T(1024)(128)(4,1)S(1)}, s32[]{:S(2)}) async-start(s8[16777216]{0:T(1024)(128)(4,1)} %bitcast.77), calls=%async_computation.7 | async-start | bytes 8388608
  173.7 10.6 %slice-start.1 = ((s8[16777216]{0:T(1024)(128)(4,1)}), s8[4194304]{0:T(1024)(128)(4,1)S(1)}, s32[]{:S(2)}) async-start(s8[16777216]{0:T(1024)(128)(4,1)} %bitcast.77), calls=%async_computation.8 | async-start | bytes 8388608
  173.9 10.5 %slice-start.2 = ((s8[16777216]{0:T(1024)(128)(4,1)}), s8[4194304]{0:T(1024)(128)(4,1)S(1)}, s32[]{:S(2)}) async-start(s8[16777216]{0:T(1024)(128)(4,1)} %bitcast.77), calls=%async_computation.9 | async-start | bytes 8388608
  178.6 5.7 %slice-start.3 = ((s8[16777216]{0:T(1024)(128)(4,1)}), s8[4194304]{0:T(1024)(128)(4,1)S(1)}, s32[]{:S(2)}) async-start(s8[16777216]{0:T(1024)(128)(4,1)} %bitcast.77), calls=%async_computation.10 | async-start | bytes 8388608
  191.4 8.9 %all-to-all-start.3 = ((f32[4,1,16384]{2,1,0:T(1,128)}), f32[4,1,16384]{2,1,0:T(1,128)S(1)}, u32[]{:S(2)}, u32[]{:S(2)}) async-start(f32[4,1,16384]{2,1,0:T(1,128)} %reshape.48), calls=%async_computation.3 | async-start | bytes 524288 | tf_op jit(solution)/shard_map/all_to_all | solution.py:110
  200.3 8.9 %all-to-all-start.4 = ((f32[4,1,16384]{2,1,0:T(1,128)}), f32[4,1,16384]{2,1,0:T(1,128)S(1)}, u32[]{:S(2)}, u32[]{:S(2)}) async-start(f32[4,1,16384]{2,1,0:T(1,128)} %reshape.50), calls=%async_computation.4 | async-start | bytes 524288 | tf_op jit(solution)/shard_map/all_to_all | solution.py:111
  216.0 51.0 %all-to-all-start.5 = ((f32[64,16,128]{2,1,0:T(8,128)}), f32[64,16,128]{2,1,0:T(8,128)S(1)}, u32[]{:S(2)}, u32[]{:S(2)}) async-start(f32[64,16,128]{2,1,0:T(8,128)} %pad_maximum_fusion.1), calls=%async_computation.5 | async-start | bytes 1048576 | tf_op jit(solution)/shard_map/all_to_all | solution.py:29
Sparse Core Ops, SparseCore 0:
  11.2 109.8 all-gather.1
where the time goes:
time: 276 us; the launch traced here: 275 us
  waiting for transfers between devices  120 us (43%)
  blocking collectives  54.1 us (20%)
  matrix products  37 us (13%)
  starting transfers between devices  18.2 us (7%)
  between operations  17 us (6%)
  local copies, waits for them, and re-layouts  16.5 us (6%)
  other arithmetic  12.8 us (5%)
    all_gather x1, waiting for transfers between devices, side_by_side(): lax.all_gather(both, axis, axis=dim, tiled=True)  110 us
    psum x4, blocking collectives, by_axis(): value = lax.psum(value, axis)  44.4 us
    dot_general x2, matrix products, on_device(): jnp.einsum('frk,fkc->frc', left_rows, whole_real, preferred_element_type=...  10.1 us
    all_to_all x1, blocking collectives, in_one_piece(): lax.all_to_all(both, axis, split_axis=split_dim, concat_axis=concat_dim,...  9.72 us
    dot_general x2, matrix products, on_device(): jnp.einsum('frk,fkc->frc', left_rows, whole_imaginary, preferred_element_...  9.44 us
    unnamed x34, local copies, waits for them, and re-layouts  8.78 us
    dot_general x16, matrix products, highest(): jnp.dot(left, right, precision=lax.Precision.HIGHEST, preferred_element_t...  8.37 us
    all_to_all x2, starting transfers between devices, on_device(): lax.all_to_all(stepped_real, 'af', split_axis=2, concat_axis=0, tiled=True)  7.41 us
  transfers between devices with their start and end apart: 6, of which 5 were waited for; matrix products, arithmetic and copies ran while one was open for 5% of the time, Pallas kernels for 0%

commit v1 on v0

--- a/solution.py
+++ b/solution.py
@@ -12,6 +12,28 @@
 AF_SA = ("af", "sa_0", "sa_1", "sa_2")
 STEP_LENGTH = 0.02
 THRESHOLD = 0.25
+
+
+def split_up(array, dim, size):
+    before, after = (array.shape[:dim], array.shape[dim + 1 :])
+    return jnp.moveaxis(array.reshape(*before, size, -1, *after), dim, 0)
+
+
+def in_order(blocks, dim):
+    dims = list(blocks.shape[1:])
+    dims[dim] *= blocks.shape[0]
+    return jnp.moveaxis(blocks, 0, dim).reshape(dims)
+
+
+def exchange_directly(x, axis, split_dim, concat_dim):
+    devices, here = (lax.axis_size(axis), lax.axis_index(axis))
+    blocks = split_up(x, split_dim, devices)
+    done = [blocks[here]]
+    for lap in range(1, devices):
+        sent = blocks[(here + lap) % devices]
+        done.append(lax.ppermute(sent, axis, [(i, (i + lap) % devices) for i in range(devices)]))
+    blocks = jnp.stack(done)[(here - jnp.arange(devices)) % devices]
+    return in_order(blocks, concat_dim)
 
 
 def side_by_side(arrays, axis, dim, along):
@@ -107,7 +129,7 @@
         stepped_real = current_real + STEP_LENGTH * gradient_real
         stepped_imaginary = current_imaginary + STEP_LENGTH * gradient_imaginary
         trace_real, trace_imaginary = (
-            lax.all_to_all(stepped_real, "af", split_axis=2, concat_axis=0, tiled=True),
+            exchange_directly(stepped_real, "af", 2, 0),
             lax.all_to_all(stepped_imaginary, "af", split_axis=2, concat_axis=0, tiled=True),
         )
         block_shape = trace_real.shape

time: 276 us -> 264 us (0.957)
  local copies, waits for them, and re-layouts: 16.5 us -> 10.7 us
  other arithmetic: 12.8 us -> 10 us
    all_to_all x2 -> x0, starting transfers between devices: 7.41 us -> none  [on_device(): lax.all_to_all(stepped_real, 'af', split_axis=2, concat_axis=0, tiled=True)]
    all_to_all x2 -> x0, waiting for transfers between devices: 6.86 us -> none  [on_device(): lax.all_to_all(stepped_real, 'af', split_axis=2, concat_axis=0, tiled=True)]
    ppermute x0 -> x6, starting transfers between devices: none -> 5.83 us  [exchange_directly(): lax.ppermute(sent, axis, [(i, (i + lap) % devices) for i in range(devices)])]
    all_to_all x2, waiting for transfers between devices: 2.54 us -> 7.48 us  [on_device(): lax.all_to_all(stepped_imaginary, 'af', split_axis=2, concat_axis=0, tile...]
    unnamed x34 -> x30, local copies, waits for them, and re-layouts: 8.78 us -> 4.54 us
  transfers between devices with their start and end apart: 6 -> 10, of which waited for: 5 -> 3; matrix products, arithmetic and copies ran while one was open for 5% -> 4% of each run, Pallas kernels for 0% -> 0%
where the time goes in v1:
time: 264 us; the launch traced here: 263 us
  waiting for transfers between devices  118 us (45%)
  blocking collectives  53.8 us (20%)
  matrix products  37 us (14%)
  starting transfers between devices  17.1 us (6%)
  between operations  17.1 us (6%)
  local copies, waits for them, and re-layouts  10.7 us (4%)
  other arithmetic  10 us (4%)
    all_gather x1, waiting for transfers between devices, side_by_side(): lax.all_gather(both, axis, axis=dim, tiled=True)  110 us
    psum x4, blocking collectives, by_axis(): value = lax.psum(value, axis)  44.5 us
    dot_general x2, matrix products, on_device(): jnp.einsum('frk,fkc->frc', left_rows, whole_real, preferred_element_type=...  10.1 us
    dot_general x2, matrix products, on_device(): jnp.einsum('frk,fkc->frc', left_rows, whole_imaginary, preferred_element_...  9.44 us
    all_to_all x1, blocking collectives, in_one_piece(): lax.all_to_all(both, axis, split_axis=split_dim, concat_axis=concat_dim,...  9.33 us
    dot_general x16, matrix products, highest(): jnp.dot(left, right, precision=lax.Precision.HIGHEST, preferred_element_t...  8.32 us
    all_to_all x2, starting transfers between devices, on_device(): lax.all_to_all(stepped_imaginary, 'af', split_axis=2, concat_axis=0, tile...  7.8 us
    all_to_all x2, waiting for transfers between devices, on_device(): lax.all_to_all(stepped_imaginary, 'af', split_axis=2, concat_axis=0, tile...  7.48 us
  transfers between devices with their start and end apart: 10, of which 3 were waited for; matrix products, arithmetic and copies ran while one was open for 4% of the time, Pallas kernels for 0%

profile of v1, /device:TPU:1, one launch (start us, length us, event | category | flops | bytes accessed | tf_op | source)
XLA Modules:
  0.0 263.3 jit_solution(12426307141581557128)
XLA Ops:
  7.2 1.7 pad_maximum_fusion.3
  11.0 110.1 %all-gather.2.cloned.1.call-done = bf16[32,512,512]{2,1,0:T(8,128)(2,1)} async-done(((bf16[32,8,512]{2,1,0:T(8,128)(2,1)}), bf16[32,512,512]{2,1,0:T(8,128)(2,1)}) %all-gather.2.cloned.1.call-update) | async-done | bytes 16777232 | tf_op jit(solution)/shard_map/all_gather | solution.py:41
  121.1 4.7 %fusion.6 = f32[16,16,512]{2,1,0:T(8,128)S(1)} fusion(bf16[32,512,512]{2,1,0:T(8,128)(2,1)} %all-gather.2.cloned.1.call-done, bf16[16,8,512]{2,1,0:T(8,128)(2,1)S(1)} %convert_element_type.67, bf16[16,8,512]{2,1,0:T(8,128)(2,1)S(1)} %convert_element_type.66), kind=kOutput, calls=%fused_computation.8 | convolution fusion | flops 134742016 | bytes 9175040 | tf_op jit(solution)/shard_map/frk,fkc->frc/dot_general | solution.py:99
  125.9 5.3 %fusion.14 = f32[16,16,512]{2,1,0:T(8,128)S(1)} fusion(bf16[32,512,512]{2,1,0:T(8,128)(2,1)} %all-gather.2.cloned.1.call-done, bf16[16,8,512]{2,1,0:T(8,128)(2,1)S(1)} %convert_element_type.67, bf16[16,8,512]{2,1,0:T(8,128)(2,1)S(1)} %convert_element_type.66), kind=kOutput, calls=%fused_computation.16 | convolution fusion | flops 134742016 | bytes 9175040 | tf_op jit(solution)/shard_map/frk,fkc->frc/dot_general | solution.py:96
  132.1 2.3 fusion.4
  134.4 2.3 fusion.12
  137.0 2.5 collective-permute-start.2
  141.5 1.5 reshape.121
  142.9 3.6 %all-to-all-start = ((f32[4,1,16384]{2,1,0:T(1,128)}), f32[4,1,16384]{2,1,0:T(1,128)S(1)}, u32[]{:S(2)}, u32[]{:S(2)}) async-start(f32[4,1,16384]{2,1,0:T(1,128)} %reshape.121), calls=%async_computation | async-start | bytes 524288 | tf_op jit(solution)/shard_map/all_to_all | solution.py:133
  148.2 3.6 %all-to-all-done = f32[4,1,16384]{2,1,0:T(1,128)S(1)} async-done(((f32[4,1,16384]{2,1,0:T(1,128)}), f32[4,1,16384]{2,1,0:T(1,128)S(1)}, u32[]{:S(2)}, u32[]{:S(2)}) %all-to-all-start) | async-done | bytes 262176 | tf_op jit(solution)/shard_map/all_to_all | solution.py:133
  158.4 9.3 %all_to_all.66 = f32[64,16,128]{2,1,0:T(8,128)S(1)} all-to-all(f32[64,16,128]{2,1,0:T(8,128)S(1)} %pad_maximum_fusion), channel_id=1, replica_groups=mesh['af'=4,'sa_0'=8,'sa_1'=4,'sa_2'=2] {'af'}, dimensions={0} | all-to-all | bytes 1048576 | tf_op jit(solution)/shard_map/all_to_all | solution.py:51
  167.8 4.7 %fusion.2 = f32[16,16,512]{2,1,0:T(8,128)S(1)} fusion(bf16[32,512,512]{2,1,0:T(8,128)(2,1)} %all-gather.2.cloned.1.call-done, bf16[16,8,512]{2,1,0:T(8,128)(2,1)S(1)} %get-tuple-element.22, bf16[16,8,512]{2,1,0:T(8,128)(2,1)S(1)} %get-tuple-element.21), kind=kOutput, calls=%fused_computation.4 | convolution fusion | flops 134742016 | bytes 9175040 | tf_op jit(solution)/shard_map/frk,fkc->frc/dot_general | solution.py:99
  172.6 4.7 %fusion.10 = f32[16,16,512]{2,1,0:T(8,128)S(1)} fusion(bf16[32,512,512]{2,1,0:T(8,128)(2,1)} %all-gather.2.cloned.1.call-done, bf16[16,8,512]{2,1,0:T(8,128)(2,1)S(1)} %get-tuple-element.22, bf16[16,8,512]{2,1,0:T(8,128)(2,1)S(1)} %get-tuple-element.21), kind=kOutput, calls=%fused_computation.12 | convolution fusion | flops 134742016 | bytes 9175040 | tf_op jit(solution)/shard_map/frk,fkc->frc/dot_general | solution.py:96
  178.2 2.3 fusion
  180.5 2.3 fusion.8
  186.1 1.5 reshape.123
  187.5 4.2 %all-to-all-start.2 = ((f32[4,1,16384]{2,1,0:T(1,128)}), f32[4,1,16384]{2,1,0:T(1,128)S(1)}, u32[]{:S(2)}, u32[]{:S(2)}) async-start(f32[4,1,16384]{2,1,0:T(1,128)} %reshape.123), calls=%async_computation.2 | async-start | bytes 524288 | tf_op jit(solution)/shard_map/all_to_all | solution.py:133
  193.4 3.9 %all-to-all-done.2 = f32[4,1,16384]{2,1,0:T(1,128)S(1)} async-done(((f32[4,1,16384]{2,1,0:T(1,128)}), f32[4,1,16384]{2,1,0:T(1,128)S(1)}, u32[]{:S(2)}, u32[]{:S(2)}) %all-to-all-start.2) | async-done | bytes 262176 | tf_op jit(solution)/shard_map/all_to_all | solution.py:133
  197.3 1.3 reduce.1
  204.1 3.5 %all-to-all-start.3 = ((f32[64,16,128]{2,1,0:T(8,128)}), f32[64,16,128]{2,1,0:T(8,128)S(1)}, u32[]{:S(2)}, u32[]{:S(2)}) async-start(f32[64,16,128]{2,1,0:T(8,128)} %pad_maximum_fusion.1), calls=%async_computation.3 | async-start | bytes 1048576 | tf_op jit(solution)/shard_map/all_to_all | solution.py:51
  210.1 9.3 %psum.28 = f32[2]{0:T(128)S(1)} all-reduce(f32[2]{0:T(128)S(1)} %pad_maximum_fusion.17), channel_id=1, replica_groups=mesh['af'=4,'sa_0'=8,'sa_1'=4,'sa_2'=2] {'af'}, use_global_device_ids=true, to_apply=%region_4.5 | all-reduce | flops 2 | bytes 16 | tf_op jit(solution)/shard_map/psum | solution.py:57
  219.3 12.5 %psum.29 = f32[2]{0:T(128)S(1)} all-reduce(f32[2]{0:T(128)S(1)} %psum.28), channel_id=1, replica_groups=mesh['af'=4,'sa_0'=8,'sa_1'=4,'sa_2'=2] {'sa_0'}, use_global_device_ids=true, to_apply=%region_5.6 | all-reduce | flops 2 | bytes 16 | tf_op jit(solution)/shard_map/psum | solution.py:57
  231.8 7.2 %psum.30 = f32[2]{0:T(128)S(1)} all-reduce(f32[2]{0:T(128)S(1)} %psum.29), channel_id=1, replica_groups=mesh['af'=4,'sa_0'=8,'sa_1'=4,'sa_2'=2] {'sa_1'}, use_global_device_ids=true, to_apply=%region_6.7 | all-reduce | flops 2 | bytes 16 | tf_op jit(solution)/shard_map/psum | solution.py:57
  239.1 15.5 %psum.31 = f32[2]{0:T(128)S(1)} all-reduce(f32[2]{0:T(128)S(1)} %psum.30), channel_id=1, replica_groups=mesh['af'=4,'sa_0'=8,'sa_1'=4,'sa_2'=2] {'sa_2'}, use_global_device_ids=true, to_apply=%region_7.8 | all-reduce | flops 2 | bytes 16 | tf_op jit(solution)/shard_map/psum | solution.py:57
  (92 shorter events, 26.4 us)
Async XLA Ops:
  7.2 114.0 %all-gather.2.cloned.1.call-start = ((), (), s32[]{:S(2)}) async-start(), calls=%async_computation.4 | async-start | bytes 17039360 | tf_op jit(solution)/shard_map/all_gather | solution.py:41
  11.0 120.2 %copy-start.1 = (f32[16,8,512]{2,1,0:T(8,128)S(1)}, f32[16,8,512]{2,1,0:T(8,128)}, u32[]{:S(2)}) copy-start(f32[16,8,512]{2,1,0:T(8,128)} %param.11) | copy-start | bytes 786436
  11.0 120.2 %copy-start.2 = (f32[16,8,512]{2,1,0:T(8,128)S(1)}, f32[16,8,512]{2,1,0:T(8,128)}, u32[]{:S(2)}) copy-start(f32[16,8,512]{2,1,0:T(8,128)} %param.10) | copy-start | bytes 786436
  11.0 120.2 %copy-start.3 = (bf16[16,8,512]{2,1,0:T(8,128)(2,1)S(1)}, bf16[16,8,512]{2,1,0:T(8,128)(2,1)}, u32[]{:S(2)}) copy-start(bf16[16,8,512]{2,1,0:T(8,128)(2,1)} %param.7) | copy-start | bytes 393220
  11.0 120.2 %copy-start.4 = (bf16[16,8,512]{2,1,0:T(8,128)(2,1)S(1)}, bf16[16,8,512]{2,1,0:T(8,128)(2,1)}, u32[]{:S(2)}) copy-start(bf16[16,8,512]{2,1,0:T(8,128)(2,1)} %param.6) | copy-start | bytes 393220
  11.0 120.2 %copy-start.5 = (f32[16]{0:T(128)S(1)}, f32[16]{0:T(128)}, u32[]{:S(2)}) copy-start(f32[16]{0:T(128)} %param.9) | copy-start | bytes 196
  11.0 120.2 %copy-start.6 = (f32[16]{0:T(128)S(1)}, f32[16]{0:T(128)}, u32[]{:S(2)}) copy-start(f32[16]{0:T(128)} %param.8) | copy-start | bytes 196
  121.1 11.0 %copy-start = (bf16[32,512,512]{2,1,0:T(8,128)(2,1)S(1)}, bf16[32,512,512]{2,1,0:T(8,128)(2,1)}, u32[]{:S(2)}) copy-start(bf16[32,512,512]{2,1,0:T(8,128)(2,1)} %all-gather.2.cloned.1.call-done) | copy-start | bytes 50331652
  137.0 9.6 %collective-permute-start.2 = (f32[16,8,128]{2,1,0:T(8,128)S(1)}, f32[16,8,128]{2,1,0:T(8,128)S(1)}, u32[]{:S(2)}, u32[]{:S(2)}) collective-permute-start(f32[16,8,128]{2,1,0:T(8,128)S(1)} %get-tuple-element.28), channel_id=1, source_target_pairs={{0,192},{64,0},{128,64},{192,128},{1,193},{65,1},{129,65},{193,129... | collective-permute-start | bytes 196616 | tf_op jit(solution)/shard_map/ppermute | solution.py:34
  139.5 7.0 %collective-permute-start.1 = (f32[16,8,128]{2,1,0:T(8,128)S(1)}, f32[16,8,128]{2,1,0:T(8,128)S(1)}, u32[]{:S(2)}, u32[]{:S(2)}) collective-permute-start(f32[16,8,128]{2,1,0:T(8,128)S(1)} %get-tuple-element.29), channel_id=1, source_target_pairs={{0,128},{64,192},{128,0},{192,64},{1,129},{65,193},{129,1},{193,65... | collective-permute-start | bytes 196616 | tf_op jit(solution)/shard_map/ppermute | solution.py:34
  140.1 6.5 %collective-permute-start = (f32[16,8,128]{2,1,0:T(8,128)S(1)}, f32[16,8,128]{2,1,0:T(8,128)S(1)}, u32[]{:S(2)}, u32[]{:S(2)}) collective-permute-start(f32[16,8,128]{2,1,0:T(8,128)S(1)} %get-tuple-element.30), channel_id=1, source_target_pairs={{0,64},{64,128},{128,192},{192,0},{1,65},{65,129},{129,193},{193,1... | collective-permute-start | bytes 196616 | tf_op jit(solution)/shard_map/ppermute | solution.py:34
  142.9 8.9 %all-to-all-start = ((f32[4,1,16384]{2,1,0:T(1,128)}), f32[4,1,16384]{2,1,0:T(1,128)S(1)}, u32[]{:S(2)}, u32[]{:S(2)}) async-start(f32[4,1,16384]{2,1,0:T(1,128)} %reshape.121), calls=%async_computation | async-start | bytes 524288 | tf_op jit(solution)/shard_map/all_to_all | solution.py:133
  155.1 23.1 %slice-start = ((s8[16777216]{0:T(1024)(128)(4,1)}), s8[4194304]{0:T(1024)(128)(4,1)S(1)}, s32[]{:S(2)}) async-start(s8[16777216]{0:T(1024)(128)(4,1)} %bitcast.97), calls=%async_computation.5 | async-start | bytes 8388608
  167.7 10.5 %slice-start.1 = ((s8[16777216]{0:T(1024)(128)(4,1)}), s8[4194304]{0:T(1024)(128)(4,1)S(1)}, s32[]{:S(2)}) async-start(s8[16777216]{0:T(1024)(128)(4,1)} %bitcast.97), calls=%async_computation.6 | async-start | bytes 8388608
  167.8 10.4 %slice-start.2 = ((s8[16777216]{0:T(1024)(128)(4,1)}), s8[4194304]{0:T(1024)(128)(4,1)S(1)}, s32[]{:S(2)}) async-start(s8[16777216]{0:T(1024)(128)(4,1)} %bitcast.97), calls=%async_computation.7 | async-start | bytes 8388608
  172.6 5.7 %slice-start.3 = ((s8[16777216]{0:T(1024)(128)(4,1)}), s8[4194304]{0:T(1024)(128)(4,1)S(1)}, s32[]{:S(2)}) async-start(s8[16777216]{0:T(1024)(128)(4,1)} %bitcast.97), calls=%async_computation.8 | async-start | bytes 8388608
  183.1 8.7 %collective-permute-start.5 = (f32[16,8,128]{2,1,0:T(8,128)S(1)}, f32[16,8,128]{2,1,0:T(8,128)S(1)}, u32[]{:S(2)}, u32[]{:S(2)}) collective-permute-start(f32[16,8,128]{2,1,0:T(8,128)S(1)} %get-tuple-element.24), channel_id=1, source_target_pairs={{0,192},{64,0},{128,64},{192,128},{1,193},{65,1},{129,65},{193,129... | collective-permute-start | bytes 196616 | tf_op jit(solution)/shard_map/ppermute | solution.py:34
  184.1 7.7 %collective-permute-start.4 = (f32[16,8,128]{2,1,0:T(8,128)S(1)}, f32[16,8,128]{2,1,0:T(8,128)S(1)}, u32[]{:S(2)}, u32[]{:S(2)}) collective-permute-start(f32[16,8,128]{2,1,0:T(8,128)S(1)} %get-tuple-element.25), channel_id=1, source_target_pairs={{0,128},{64,192},{128,0},{192,64},{1,129},{65,193},{129,1},{193,65... | collective-permute-start | bytes 196616 | tf_op jit(solution)/shard_map/ppermute | solution.py:34
  185.2 6.5 %collective-permute-start.3 = (f32[16,8,128]{2,1,0:T(8,128)S(1)}, f32[16,8,128]{2,1,0:T(8,128)S(1)}, u32[]{:S(2)}, u32[]{:S(2)}) collective-permute-start(f32[16,8,128]{2,1,0:T(8,128)S(1)} %get-tuple-element.26), channel_id=1, source_target_pairs={{0,64},{64,128},{128,192},{192,0},{1,65},{65,129},{129,193},{193,1... | collective-permute-start | bytes 196616 | tf_op jit(solution)/shard_map/ppermute | solution.py:34
  187.5 9.7 %all-to-all-start.2 = ((f32[4,1,16384]{2,1,0:T(1,128)}), f32[4,1,16384]{2,1,0:T(1,128)S(1)}, u32[]{:S(2)}, u32[]{:S(2)}) async-start(f32[4,1,16384]{2,1,0:T(1,128)} %reshape.123), calls=%async_computation.2 | async-start | bytes 524288 | tf_op jit(solution)/shard_map/all_to_all | solution.py:133
  204.1 51.0 %all-to-all-start.3 = ((f32[64,16,128]{2,1,0:T(8,128)}), f32[64,16,128]{2,1,0:T(8,128)S(1)}, u32[]{:S(2)}, u32[]{:S(2)}) async-start(f32[64,16,128]{2,1,0:T(8,128)} %pad_maximum_fusion.1), calls=%async_computation.3 | async-start | bytes 1048576 | tf_op jit(solution)/shard_map/all_to_all | solution.py:51
Sparse Core Ops, SparseCore 0:
  11.2 109.8 all-gather.1
